TPU v7x, 32 devices: a whole 2x2x4 slice. The times are simulated.
32 devices in a mesh: tp: 8 (over z, core), fs: 4 (over y, x).
Axes of the slice: x: 2, y: 2, z: 4, core: 2. Of those that a mesh axis runs over, the one named last changes fastest.
Arguments:
- tokens: bfloat16 [128, 8192], P(('tp', 'fs')), may hold values from -6 to 6
- gate_weight: bfloat16 [8192, 29568], P('fs', 'tp'), may hold values from -0.0625 to 0.0625
- up_weight: bfloat16 [8192, 29568], P('fs', 'tp'), may hold values from -0.0625 to 0.0625
- down_weight: bfloat16 [29568, 8192], P('tp', 'fs'), may hold values from -0.046875 to 0.046875
Outputs:
- mixed: bfloat16 [128, 8192], P(None, ('fs', 'tp'))
All inputs are finite; a program needn't handle non-finite values.
Results may differ from a plain program's by a relative error of at most 0.0049.
Values may be sent and summed in bfloat16 or wider, within the bound.
A program may use at most 128 MiB of HBM per device.

v0:
```python
import jax
import jax.numpy as jnp
from jax import lax
from jax.sharding import PartitionSpec as P


def body(tokens, gate_weight, up_weight, down_weight):
    by_feature = lax.all_to_all(tokens, "fs", split_axis=1, concat_axis=0, tiled=True)
    feature_rows = lax.all_gather(by_feature, "tp", axis=0, tiled=True)
    gate_part = jnp.dot(feature_rows, gate_weight, preferred_element_type=jnp.float32)
    up_part = jnp.dot(feature_rows, up_weight, preferred_element_type=jnp.float32)
    gate, up = (
        lax.psum_scatter(gate_part, "fs", scatter_dimension=1, tiled=True),
        lax.psum_scatter(up_part, "fs", scatter_dimension=1, tiled=True),
    )
    hidden = (jax.nn.silu(gate) * up).astype(jnp.bfloat16)
    hidden_all = lax.all_gather(hidden, "fs", axis=1, tiled=True)
    partial_out = jnp.dot(hidden_all, down_weight, preferred_element_type=jnp.float32)
    summed = lax.psum_scatter(partial_out, "tp", scatter_dimension=1, tiled=True)
    return summed.astype(jnp.bfloat16)


def solution(mesh):
    return jax.shard_map(
        body,
        mesh=mesh,
        in_specs=(P(("tp", "fs"), None), P("fs", "tp"), P("fs", "tp"), P("tp", "fs")),
        out_specs=P(None, ("fs", "tp")),
        check_vma=False,
    )
```

profile of v0, /device:TPU:0, one launch (start us, length us, event | category | flops | bytes accessed | tf_op | source)
XLA Modules:
  0.0 184.2 jit_solution(5929641926974322343)
XLA Ops:
  6.5 0.0 reduce-scatter.6.cloned.1.call-start
  6.5 10.0 %all_to_all.19 = bf16[4,4,2048]{2,0,1:T(4,128)(2,1)S(1)} all-to-all(bf16[4,4,2048]{2,0,1:T(4,128)(2,1)} %bitcast.19), channel_id=1, replica_groups=mesh['tp'=8,'fs'=4] {'fs'}, dimensions={1} | all-to-all | bytes 131072 | tf_op jit(solution)/shard_map/all_to_all | solution.py:8
  16.6 0.0 copy-start
  16.6 15.1 %all_gather.6 = bf16[128,2048]{1,0:T(8,128)(2,1)S(1)} all-gather(bf16[16,2048]{1,0:T(8,128)(2,1)S(1)} %all_to_all.17), channel_id=1, replica_groups=mesh['tp'=8,'fs'=4] {'tp'}, dimensions={0}, use_global_device_ids=true | all-gather | bytes 589824 | tf_op jit(solution)/shard_map/all_gather | solution.py:9
  31.8 7.6 %fusion.5 = f32[128,3696]{0,1:T(8,128)S(1)} fusion(bf16[128,2048]{1,0:T(8,128)(2,1)S(1)} %all_gather.6, bf16[2048,3696]{0,1:T(8,128)(2,1)} %param.5), kind=kOutput, calls=%fused_computation.3 | convolution fusion | flops 1937768448 | bytes 17555456 | tf_op jit(solution)/shard_map/dot_general | solution.py:10
  39.3 0.0 copy-done
  39.3 0.0 copy-start.1
  39.4 5.6 %fusion.6 = f32[128,3696]{0,1:T(8,128)} fusion(bf16[128,2048]{1,0:T(8,128)(2,1)S(1)} %all_gather.6, bf16[2048,3696]{0,1:T(8,128)(2,1)S(1)} %copy-done), kind=kOutput, calls=%fused_computation.4 | convolution fusion | flops 1937768448 | bytes 17555456 | tf_op jit(solution)/shard_map/dot_general | solution.py:11
  44.9 67.6 %fusion.4 = (f32[128,928]{0,1:T(8,128)S(1)}, f32[128,928]{0,1:T(8,128)S(1)}) fusion(f32[128,3696]{0,1:T(8,128)} %fusion.6, f32[128,3696]{0,1:T(8,128)S(1)} %fusion.5), kind=kCustom, calls=%all-reduce-scatter.2 | all-reduce-scatter fusion | flops 950273 | bytes 4735488
  112.6 1.7 collective-permute-start
  114.3 4.3 %collective-permute-start.1 = (f32[128,12]{0,1:T(8,128)S(1)}, f32[128,12]{0,1:T(8,128)S(1)}, u32[]{:S(2)}, u32[]{:S(2)}) collective-permute-start(f32[128,12]{0,1:T(8,128)S(1)} %slice.1), channel_id=1, source_target_pairs={{0,1},{1,2},{2,3},{4,5},{5,6},{6,7},{8,9},{9,10},{10,11},{12,13},{... | collective-permute-start | bytes 18440
  118.6 0.0 copy-done.1
  118.6 0.6 dynamic-slice.6
  119.9 0.0 collective-permute-done
  119.9 1.1 concatenate
  121.0 0.0 collective-permute-done.1
  121.0 1.1 concatenate.1
  122.1 0.2 fusion.3
  122.3 12.0 %all-gather = bf16[4,924,128]{2,1,0:T(8,128)(2,1)S(1)} all-gather(bf16[1,924,128]{2,1,0:T(8,128)(2,1)S(1)} %fusion.3), channel_id=1, replica_groups=mesh['tp'=8,'fs'=4] {'fs'}, dimensions={0}, use_global_device_ids=true | all-gather | bytes 1182720 | tf_op jit(solution)/shard_map/all_gather | solution.py:17
  134.3 0.2 reshape.4
  134.5 8.5 %fusion.7 = f32[128,2048]{1,0:T(8,128)} fusion(bf16[3696,128]{1,0:T(8,128)(2,1)S(1)} %reshape.4, bf16[3696,2048]{1,0:T(8,128)(2,1)} %param.7), kind=kOutput, calls=%fused_computation.5 | convolution fusion | flops 1937768448 | bytes 17133568 | tf_op jit(solution)/shard_map/dot_general | solution.py:18
  143.0 0.0 reduce-scatter.6.cloned.1.call-update
  143.0 32.8 %reduce-scatter.6.cloned.1.call-done = f32[128,256]{1,0:T(8,128)} async-done(((f32[128,2048]{1,0:T(8,128)}), f32[128,256]{1,0:T(8,128)}) %reduce-scatter.6.cloned.1.call-update) | async-done | bytes 131088 | tf_op jit(solution)/shard_map/reduce_scatter | solution.py:19
  175.8 1.5 convert_element_type.7
  (3 shorter events, 0.0 us)
Async XLA Ops:
  6.5 169.3 %reduce-scatter.6.cloned.1.call-start = ((), (), s32[]{:S(2)}) async-start(), calls=%async_computation.2 | async-start | bytes 1179648 | tf_op jit(solution)/shard_map/reduce_scatter | solution.py:19
  16.6 22.7 %copy-start = (bf16[2048,3696]{0,1:T(8,128)(2,1)S(1)}, bf16[2048,3696]{0,1:T(8,128)(2,1)}, u32[]{:S(2)}) copy-start(bf16[2048,3696]{0,1:T(8,128)(2,1)} %param.6) | copy-start | bytes 45416452
  39.3 79.3 %copy-start.1 = (u32[32]{0:T(128)S(1)}, u32[32]{0:T(128)}, u32[]{:S(2)}) copy-start(u32[32]{0:T(128)} %constant.6) | copy-start | bytes 388
  112.6 7.3 %collective-permute-start = (f32[128,12]{0,1:T(8,128)S(1)}, f32[128,12]{0,1:T(8,128)S(1)}, u32[]{:S(2)}, u32[]{:S(2)}) collective-permute-start(f32[128,12]{0,1:T(8,128)S(1)} %slice), channel_id=1, source_target_pairs={{0,1},{1,2},{2,3},{4,5},{5,6},{6,7},{8,9},{9,10},{10,11},{12,13},{... | collective-permute-start | bytes 18440
  114.3 6.7 %collective-permute-start.1 = (f32[128,12]{0,1:T(8,128)S(1)}, f32[128,12]{0,1:T(8,128)S(1)}, u32[]{:S(2)}, u32[]{:S(2)}) collective-permute-start(f32[128,12]{0,1:T(8,128)S(1)} %slice.1), channel_id=1, source_target_pairs={{0,1},{1,2},{2,3},{4,5},{5,6},{6,7},{8,9},{9,10},{10,11},{12,13},{... | collective-permute-start | bytes 18440
Sparse Core Ops, SparseCore 0:
  143.1 32.6 reduce-scatter.5
where the time goes:
time: 185 us; the launch traced here: 184 us
  blocking collectives  105 us (57%)
  waiting for transfers between devices  32.9 us (18%)
  matrix products  21.6 us (12%)
  between operations  14.2 us (8%)
  starting transfers between devices  6.01 us (3%)
  local copies, waits for them, and re-layouts  3.02 us (2%)
    unnamed x1, blocking collectives  67.6 us
    reduce_scatter x1, waiting for transfers between devices, body(): lax.psum_scatter(partial_out, 'tp', scatter_dimension=1, tiled=True)  32.8 us
    all_gather x1, blocking collectives, body(): feature_rows = lax.all_gather(by_feature, 'tp', axis=0, tiled=True)  15.1 us
    all_gather x1, blocking collectives, body(): hidden_all = lax.all_gather(hidden, 'fs', axis=1, tiled=True)  12 us
    all_to_all x1, blocking collectives, body(): lax.all_to_all(tokens, 'fs', split_axis=1, concat_axis=0, tiled=True)  10 us
    dot_general x1, matrix products, body(): jnp.dot(hidden_all, down_weight, preferred_element_type=jnp.float32)  8.5 us
    dot_general x1, matrix products, body(): jnp.dot(feature_rows, gate_weight, preferred_element_type=jnp.float32)  7.58 us
    unnamed x2, starting transfers between devices  6.01 us
  transfers between devices with their start and end apart: 3, of which 1 were waited for; matrix products, arithmetic and copies ran while one was open for 1% of the time, Pallas kernels for 0%

commit v1 on v0

v1 whole, which is shorter than its diff:
```python
import functools

import jax
import jax.numpy as jnp
from jax import lax
from jax.experimental import pallas as pl
from jax.experimental.pallas import tpu as pltpu
from jax.sharding import PartitionSpec as P

BF16, F32 = jnp.bfloat16, jnp.float32
LANES, SUBLANES = 128, 16
CHUNK = 5 * LANES
LOADS = 4


def chunks_of(width):
    return [(at, min(CHUNK, width - at)) for at in range(0, width, CHUNK)]


def round_up(n, m):
    return (n + m - 1) // m * m


def kernel(n_tensor, n_stored, pieces, tok_ref, gate_hbm, up_hbm, down_hbm, out_ref,
           gate_w, up_w, down_w, blocks, x, part, own, rs_send, rs_recv, hid,
           acc, keep, pair_send, pair_recv, z_send, z_recv,
           load_sem, a_send, a_recv, b_send, b_recv, c_send, c_recv,
           rs_ssem, rs_rsem, ag_ssem, ag_rsem, p_ssem, p_rsem, z_ssem, z_rsem):
    tp, fs = lax.axis_index("tp"), lax.axis_index("fs")
    core, chip = lax.rem(tp, 2), tp // 2
    partner = tp + 1 - 2 * core
    n_chips = n_tensor // 2
    width = gate_w.shape[1]
    chunks = chunks_of(width)
    rows = own.shape[2]
    total = rows * n_stored
    lane_w = keep.shape[2]

    loads = []
    for i, (hbm, vmem) in enumerate(((gate_hbm, gate_w), (up_hbm, up_w), (down_hbm, down_w))):
        depth = hbm.shape[0]
        step = round_up((depth + LOADS - 1) // LOADS, SUBLANES)
        for j, at in enumerate(range(0, depth, step)):
            span = pl.ds(at, min(step, depth - at))
            copy = pltpu.make_async_copy(hbm.at[span, :], vmem.at[span, :], load_sem.at[i, j])
            copy.start()
            loads.append((i, copy))

    def remote(src, dst, ssem, rsem, tensor, stored):
        return pltpu.make_async_remote_copy(
            src_ref=src, dst_ref=dst, send_sem=ssem, recv_sem=rsem,
            device_id={"tp": tensor, "fs": stored},
            device_id_type=pl.DeviceIdType.MESH)

    others = [lax.rem(fs + j, n_stored) for j in range(1, n_stored)]
    sources = [lax.rem(fs + n_stored - j, n_stored) for j in range(1, n_stored)]
    chips = [lax.rem(chip + j, n_chips) for j in range(1, n_chips)]
    chip_sources = [lax.rem(chip + n_chips - j, n_chips) for j in range(1, n_chips)]

    barrier = pltpu.get_barrier_semaphore()
    peers = [(tp, f) for f in others] + [(2 * d + core, fs) for d in chips] + [(partner, fs)]
    for tensor, stored in peers:
        pl.semaphore_signal(barrier, inc=1, device_id={"tp": tensor, "fs": stored},
                            device_id_type=pl.DeviceIdType.MESH)
    blocks[tp, fs] = tok_ref[fs]
    pl.semaphore_wait(barrier, len(peers))

    sends = []
    for j, f in enumerate(others):
        copy = remote(tok_ref.at[f], blocks.at[tp, fs], a_send.at[j], a_recv.at[j], tp, f)
        copy.start()
        sends.append(copy)
    for j in range(n_stored - 1):
        sends[j].wait_recv()
    mid = []
    for j, d in enumerate(chips):
        copy = remote(blocks.at[tp], blocks.at[tp], b_send.at[j], b_recv.at[j],
                      2 * d + core, fs)
        copy.start()
        mid.append(copy)
    first = remote(blocks.at[tp], blocks.at[tp], c_send.at[0], c_recv.at[0], partner, fs)
    first.start()
    side = [first]
    for j, d in enumerate(chip_sources):
        mid[j].wait_recv()
        got = 2 * d + core
        copy = remote(blocks.at[got], blocks.at[got], c_send.at[j + 1], c_recv.at[j + 1],
                      partner, fs)
        copy.start()
        side.append(copy)
    for copy in side:
        copy.wait_recv()

    per = blocks.shape[1] * blocks.shape[2]
    cols = blocks.shape[3]
    group = 256 // pieces
    row_id = lax.broadcasted_iota(jnp.int32, (group, 256), 0)
    col_id = lax.broadcasted_iota(jnp.int32, (group, 256), 1)
    picks = [(col_id == row_id * pieces + q).astype(F32).astype(BF16) for q in range(pieces)]
    n_blocks = 256 // per
    for g in range(total // group):
        flat = blocks[g * n_blocks:(g + 1) * n_blocks].reshape(256, cols)
        for q in range(pieces):
            x[g * group:(g + 1) * group, q * cols:(q + 1) * cols] = jnp.dot(
                picks[q], flat, preferred_element_type=F32).astype(BF16)
    for copy in sends + mid + side:
        copy.wait_send()

    for i, copy in loads:
        if i < 2:
            copy.wait()

    rs = []
    for c, (at, size) in enumerate(chunks):
        for k, w in enumerate((gate_w, up_w)):
            value = jnp.dot(x[...], w[:, at:at + size], preferred_element_type=F32)
            if size < CHUNK:
                part[k] = jnp.zeros_like(part[k])
            part[k, :, :size] = value
            for f in range(n_stored):
                rs_send[c, f, k] = part[k, f * rows:(f + 1) * rows, :].astype(BF16)
            own[c, k] = part[k, pl.ds(pl.multiple_of(fs * rows, rows), rows), :]
        padded = min(CHUNK, round_up(size, LANES))
        copies = []
        for j, f in enumerate(others):
            copy = remote(rs_send.at[c, f, :, :, pl.ds(0, padded)],
                          rs_recv.at[c, fs, :, :, pl.ds(0, padded)],
                          rs_ssem.at[c, j], rs_rsem.at[c, j], tp, f)
            copy.start()
            copies.append(copy)
        rs.append(copies)

    def reduce(c):
        size = chunks[c][1]
        padded = min(CHUNK, round_up(size, LANES))
        gate, up = own[c, 0, :, :padded], own[c, 1, :, :padded]
        for j, f in enumerate(sources):
            rs[c][j].wait_recv()
            gate = gate + rs_recv[c, f, 0, :, :padded].astype(F32)
            up = up + rs_recv[c, f, 1, :, :padded].astype(F32)
        hid[c, fs, :, :padded] = (gate / (1.0 + jnp.exp(-gate)) * up).astype(BF16)
        copies = []
        for j, f in enumerate(others):
            copy = remote(hid.at[c, fs, :, pl.ds(0, padded)], hid.at[c, fs, :, pl.ds(0, padded)],
                          ag_ssem.at[c, j], ag_rsem.at[c, j], tp, f)
            copy.start()
            copies.append(copy)
        return copies

    def down(c, d):
        at, size = chunks[c]
        h = hid[c].reshape(total, CHUNK)[:, :size]
        return jnp.dot(h, down_w[at:at + size, d * 2 * lane_w:(d + 1) * 2 * lane_w],
                       preferred_element_type=F32)

    ag = []
    last = len(chunks) - 1
    for c in range(last + 1):
        ag.append(reduce(c))
    for i, copy in loads:
        if i == 2:
            copy.wait()
    pair = []
    for c in range(last + 1):
        for copy in ag[c]:
            copy.wait_recv()
        for d in range(n_chips):
            span = slice(d * 2 * lane_w, (d + 1) * 2 * lane_w)
            value = down(c, d)
            if c > 0:
                value = value + acc[:, span]
            if c < last:
                acc[:, span] = value
                continue
            low, high = value[:, :lane_w], value[:, lane_w:]
            keep[d] = jnp.where(core == 0, low, high)
            pair_send[d] = jnp.where(core == 0, high, low)
            copy = remote(pair_send.at[d], pair_recv.at[d], p_ssem.at[d], p_rsem.at[d],
                          partner, fs)
            copy.start()
            pair.append(copy)

    for d in range(n_chips):
        pair[d].wait_recv()
        value = keep[d] + pair_recv[d]
        keep[d] = value
        z_send[d] = value.astype(BF16)
    final = []
    for j, d in enumerate(chips):
        copy = remote(z_send.at[d], z_recv.at[chip], z_ssem.at[j], z_rsem.at[j],
                      2 * d + core, fs)
        copy.start()
        final.append(copy)
    value = keep[chip]
    for j, d in enumerate(chip_sources):
        final[j].wait_recv()
        value = value + z_recv[d].astype(F32)
    out_ref[...] = value.astype(BF16)

    for copy in [q for c in rs + ag for q in c] + pair + final:
        copy.wait_send()


def body(tokens, gate_weight, up_weight, down_weight):
    n_tensor, n_stored = lax.axis_size("tp"), lax.axis_size("fs")
    mine, model = tokens.shape
    depth, width = gate_weight.shape
    total = mine * n_tensor * n_stored
    pieces = max(1, SUBLANES // mine)
    cols = depth // pieces
    lane_w = depth // n_tensor
    n_chips = n_tensor // 2
    tok = tokens.reshape(mine, n_stored, pieces, cols).transpose(1, 0, 2, 3)
    tok = tok.reshape(n_stored, mine * pieces, cols)
    n_chunks = len(chunks_of(width))
    rows = total // n_stored
    dma = pltpu.SemaphoreType.DMA
    any_space = pl.BlockSpec(memory_space=pl.ANY)
    vmem = pl.BlockSpec(memory_space=pltpu.VMEM)
    return pl.pallas_call(
        functools.partial(kernel, n_tensor, n_stored, pieces),
        out_shape=jax.ShapeDtypeStruct((total, lane_w), BF16),
        in_specs=[vmem, any_space, any_space, any_space],
        out_specs=vmem,
        scratch_shapes=[
            pltpu.VMEM(gate_weight.shape, BF16),
            pltpu.VMEM(up_weight.shape, BF16),
            pltpu.VMEM(down_weight.shape, BF16),
            pltpu.VMEM((n_tensor, n_stored, mine * pieces, cols), BF16),
            pltpu.VMEM((total, depth), BF16),
            pltpu.VMEM((2, total, CHUNK), F32),
            pltpu.VMEM((n_chunks, 2, rows, CHUNK), F32),
            pltpu.VMEM((n_chunks, n_stored, 2, rows, CHUNK), BF16),
            pltpu.VMEM((n_chunks, n_stored, 2, rows, CHUNK), BF16),
            pltpu.VMEM((n_chunks, n_stored, rows, CHUNK), BF16),
            pltpu.VMEM((total, down_weight.shape[1]), F32),
            pltpu.VMEM((n_chips, total, lane_w), F32),
            pltpu.VMEM((n_chips, total, lane_w), F32),
            pltpu.VMEM((n_chips, total, lane_w), F32),
            pltpu.VMEM((n_chips, total, lane_w), BF16),
            pltpu.VMEM((n_chips, total, lane_w), BF16),
            dma((3, LOADS)),
            dma((n_stored,)), dma((n_stored,)),
            dma((n_chips,)), dma((n_chips,)),
            dma((n_chips,)), dma((n_chips,)),
            dma((n_chunks, n_stored)), dma((n_chunks, n_stored)),
            dma((n_chunks, n_stored)), dma((n_chunks, n_stored)),
            dma((n_chips,)), dma((n_chips,)),
            dma((n_chips,)), dma((n_chips,)),
        ],
        compiler_params=pltpu.CompilerParams(
            collective_id=0, has_side_effects=True, vmem_limit_bytes=62 * 2**20),
    )(tok, gate_weight, up_weight, down_weight)


def solution(mesh):
    return jax.shard_map(
        body,
        mesh=mesh,
        in_specs=(P(("tp", "fs"), None), P("fs", "tp"), P("fs", "tp"), P("tp", "fs")),
        out_specs=P(None, ("fs", "tp")),
        check_vma=False,
    )
```

time: 185 us -> 103 us (0.56)
  blocking collectives: 105 us -> 0 us
  Pallas kernels: 0 us -> 60.6 us
  local copies, waits for them, and re-layouts: 3.02 us -> 41.2 us
  waiting for transfers between devices: 32.9 us -> 0 us
  matrix products: 21.6 us -> 0 us
  between operations: 14.2 us -> 0.02 us
  starting transfers between devices: 6.01 us -> 0 us
    unnamed x1 -> x0, blocking collectives: 67.6 us -> none
    pallas_call x0 -> x1, Pallas kernels: none -> 60.6 us  [body(): pl.pallas_call(functools.partial(kernel, n_tensor, n_stored, pieces), out...]
    unnamed x10 -> x3, local copies, waits for them, and re-layouts: 3 us -> 39.7 us
    reduce_scatter x1 -> x0, waiting for transfers between devices: 32.8 us -> none  [body(): lax.psum_scatter(partial_out, 'tp', scatter_dimension=1, tiled=True)]
    all_gather x2 -> x0, blocking collectives: 27.1 us -> none  [the longest x1 15.1 us: body(): feature_rows = lax.all_gather(by_feature, 'tp', axis=0, tiled=True)]
    dot_general x3 -> x0, matrix products: 21.6 us -> none  [the longest x1 8.5 us: body(): jnp.dot(hidden_all, down_weight, preferred_element_type=jnp.float32)]
    all_to_all x1 -> x0, blocking collectives: 10 us -> none  [body(): lax.all_to_all(tokens, 'fs', split_axis=1, concat_axis=0, tiled=True)]
    unnamed x2 -> x0, starting transfers between devices: 6.01 us -> none
  transfers between devices with their start and end apart: 3 -> 0, of which waited for: 1 -> 0; matrix products, arithmetic and copies ran while one was open for 1% -> 0% of each run, Pallas kernels for 0% -> 0%
where the time goes in v1:
time: 103 us; the launch traced here: 102 us
  Pallas kernels  60.6 us (59%)
  local copies, waits for them, and re-layouts  41.2 us (40%)
    pallas_call x1, Pallas kernels, body(): pl.pallas_call(functools.partial(kernel, n_tensor, n_stored, pieces), out...  60.6 us
    unnamed x3, local copies, waits for them, and re-layouts  39.7 us

profile of v1, /device:TPU:0, one launch (start us, length us, event | category | flops | bytes accessed | tf_op | source)
XLA Modules:
  0.0 101.8 jit_solution(11646410449005294955)
XLA Ops:
  0.0 0.9 reshape.6
  0.9 0.6 reshape.7.tok_ref
  1.6 19.1 %copy.6.gate_hbm = bf16[2048,3696]{1,0:T(8,128)(2,1)} copy(bf16[2048,3696]{0,1:T(8,128)(2,1)} %param.5) | data formatting | bytes 30277632 | tf_op args[1]
  20.7 19.1 %copy.7.up_hbm = bf16[2048,3696]{1,0:T(8,128)(2,1)} copy(bf16[2048,3696]{0,1:T(8,128)(2,1)} %param.6) | data formatting | bytes 30277632 | tf_op args[2]
  39.8 60.6 %shard_map.46 = bf16[128,256]{1,0:T(8,128)(2,1)} custom-call(bf16[4,16,512]{2,1,0:T(8,128)(2,1)} %reshape.7.tok_ref, bf16[2048,3696]{1,0:T(8,128)(2,1)} %copy.6.gate_hbm, bf16[2048,3696]{1,0:T(8,128)(2,1)} %copy.7.up_hbm, bf16[3696,2048]{1,0:T(8,128)(2,1)} %down_hbm.1), custom_call_target="tpu_custom_call" | custom-call | tf_op jit(solution)/shard_map/pallas_call | solution.py:220
  100.4 1.5 %copy.11 = bf16[128,256]{1,0:T(8,128)(2,1)} copy(bf16[128,256]{1,0:T(8,128)(2,1)} %shard_map.46) | data formatting | bytes 131072
  (1 shorter events, 0.0 us)

commit v2 on v1

--- a/solution.py
+++ b/solution.py
@@ -10,11 +10,15 @@
 BF16, F32 = jnp.bfloat16, jnp.float32
 LANES, SUBLANES = 128, 16
 CHUNK = 5 * LANES
-LOADS = 4
 
 
 def chunks_of(width):
-    return [(at, min(CHUNK, width - at)) for at in range(0, width, CHUNK)]
+    out, at = [], 0
+    for size in (256, 512):
+        if at + size < width:
+            out.append((at, size))
+            at += size
+    return out + [(q, min(CHUNK, width - q)) for q in range(at, width, CHUNK)]
 
 
 def round_up(n, m):
@@ -30,21 +34,22 @@
     core, chip = lax.rem(tp, 2), tp // 2
     partner = tp + 1 - 2 * core
     n_chips = n_tensor // 2
-    width = gate_w.shape[1]
+    width = gate_w.shape[0]
     chunks = chunks_of(width)
-    rows = own.shape[2]
-    total = rows * n_stored
+    total = x.shape[0]
     lane_w = keep.shape[2]
 
-    loads = []
+    loads = {}
     for i, (hbm, vmem) in enumerate(((gate_hbm, gate_w), (up_hbm, up_w), (down_hbm, down_w))):
-        depth = hbm.shape[0]
-        step = round_up((depth + LOADS - 1) // LOADS, SUBLANES)
-        for j, at in enumerate(range(0, depth, step)):
-            span = pl.ds(at, min(step, depth - at))
-            copy = pltpu.make_async_copy(hbm.at[span, :], vmem.at[span, :], load_sem.at[i, j])
-            copy.start()
-            loads.append((i, copy))
+        for c, (at, size) in enumerate(chunks):
+            span = pl.ds(at, size)
+            loads[i, c] = pltpu.make_async_copy(
+                hbm.at[span, :], vmem.at[span, :], load_sem.at[i, c])
+    for c in range(len(chunks)):
+        loads[0, c].start()
+        loads[1, c].start()
+    for c in range(len(chunks)):
+        loads[2, c].start()
 
     def remote(src, dst, ssem, rsem, tensor, stored):
         return pltpu.make_async_remote_copy(
@@ -106,42 +111,42 @@
     for copy in sends + mid + side:
         copy.wait_send()
 
-    for i, copy in loads:
-        if i < 2:
-            copy.wait()
+    def share(c):
+        return round_up(chunks[c][1], SUBLANES * n_stored) // n_stored
 
     rs = []
     for c, (at, size) in enumerate(chunks):
+        sub = share(c)
         for k, w in enumerate((gate_w, up_w)):
-            value = jnp.dot(x[...], w[:, at:at + size], preferred_element_type=F32)
-            if size < CHUNK:
-                part[k] = jnp.zeros_like(part[k])
-            part[k, :, :size] = value
+            loads[k, c].wait()
+            part[k, :size, :] = lax.dot_general(
+                w[at:at + size, :], x[...], (((1,), (1,)), ((), ())),
+                preferred_element_type=F32)
+            if size < sub * n_stored:
+                part[k, size:sub * n_stored, :] = jnp.zeros((sub * n_stored - size, total), F32)
             for f in range(n_stored):
-                rs_send[c, f, k] = part[k, f * rows:(f + 1) * rows, :].astype(BF16)
-            own[c, k] = part[k, pl.ds(pl.multiple_of(fs * rows, rows), rows), :]
-        padded = min(CHUNK, round_up(size, LANES))
+                rs_send[c, f, k, :sub, :] = part[k, f * sub:(f + 1) * sub, :].astype(BF16)
+            own[c, k, :sub, :] = part[k, pl.ds(pl.multiple_of(fs * sub, sub), sub), :]
         copies = []
         for j, f in enumerate(others):
-            copy = remote(rs_send.at[c, f, :, :, pl.ds(0, padded)],
-                          rs_recv.at[c, fs, :, :, pl.ds(0, padded)],
+            copy = remote(rs_send.at[c, f, :, pl.ds(0, sub), :],
+                          rs_recv.at[c, fs, :, pl.ds(0, sub), :],
                           rs_ssem.at[c, j], rs_rsem.at[c, j], tp, f)
             copy.start()
             copies.append(copy)
         rs.append(copies)
 
     def reduce(c):
-        size = chunks[c][1]
-        padded = min(CHUNK, round_up(size, LANES))
-        gate, up = own[c, 0, :, :padded], own[c, 1, :, :padded]
+        sub = share(c)
+        gate, up = own[c, 0, :sub, :], own[c, 1, :sub, :]
         for j, f in enumerate(sources):
             rs[c][j].wait_recv()
-            gate = gate + rs_recv[c, f, 0, :, :padded].astype(F32)
-            up = up + rs_recv[c, f, 1, :, :padded].astype(F32)
-        hid[c, fs, :, :padded] = (gate / (1.0 + jnp.exp(-gate)) * up).astype(BF16)
+            gate = gate + rs_recv[c, f, 0, :sub, :].astype(F32)
+            up = up + rs_recv[c, f, 1, :sub, :].astype(F32)
+        hid[c, fs, :sub, :] = (gate / (1.0 + jnp.exp(-gate)) * up).astype(BF16)
         copies = []
         for j, f in enumerate(others):
-            copy = remote(hid.at[c, fs, :, pl.ds(0, padded)], hid.at[c, fs, :, pl.ds(0, padded)],
+            copy = remote(hid.at[c, fs, pl.ds(0, sub), :], hid.at[c, fs, pl.ds(0, sub), :],
                           ag_ssem.at[c, j], ag_rsem.at[c, j], tp, f)
             copy.start()
             copies.append(copy)
@@ -149,19 +154,18 @@
 
     def down(c, d):
         at, size = chunks[c]
-        h = hid[c].reshape(total, CHUNK)[:, :size]
-        return jnp.dot(h, down_w[at:at + size, d * 2 * lane_w:(d + 1) * 2 * lane_w],
-                       preferred_element_type=F32)
+        sub = share(c)
+        h = hid[c, :, :sub, :].reshape(n_stored * sub, total)[:size]
+        w = down_w[at:at + size, d * 2 * lane_w:(d + 1) * 2 * lane_w]
+        return lax.dot_general(h, w, (((0,), (0,)), ((), ())), preferred_element_type=F32)
 
     ag = []
     last = len(chunks) - 1
     for c in range(last + 1):
         ag.append(reduce(c))
-    for i, copy in loads:
-        if i == 2:
-            copy.wait()
     pair = []
     for c in range(last + 1):
+        loads[2, c].wait()
         for copy in ag[c]:
             copy.wait_recv()
         for d in range(n_chips):
@@ -213,7 +217,7 @@
     tok = tokens.reshape(mine, n_stored, pieces, cols).transpose(1, 0, 2, 3)
     tok = tok.reshape(n_stored, mine * pieces, cols)
     n_chunks = len(chunks_of(width))
-    rows = total // n_stored
+    most = CHUNK // n_stored
     dma = pltpu.SemaphoreType.DMA
     any_space = pl.BlockSpec(memory_space=pl.ANY)
     vmem = pl.BlockSpec(memory_space=pltpu.VMEM)
@@ -223,23 +227,23 @@
         in_specs=[vmem, any_space, any_space, any_space],
         out_specs=vmem,
         scratch_shapes=[
-            pltpu.VMEM(gate_weight.shape, BF16),
-            pltpu.VMEM(up_weight.shape, BF16),
+            pltpu.VMEM((width, depth), BF16),
+            pltpu.VMEM((width, depth), BF16),
             pltpu.VMEM(down_weight.shape, BF16),
             pltpu.VMEM((n_tensor, n_stored, mine * pieces, cols), BF16),
             pltpu.VMEM((total, depth), BF16),
-            pltpu.VMEM((2, total, CHUNK), F32),
-            pltpu.VMEM((n_chunks, 2, rows, CHUNK), F32),
-            pltpu.VMEM((n_chunks, n_stored, 2, rows, CHUNK), BF16),
-            pltpu.VMEM((n_chunks, n_stored, 2, rows, CHUNK), BF16),
-            pltpu.VMEM((n_chunks, n_stored, rows, CHUNK), BF16),
+            pltpu.VMEM((2, CHUNK, total), F32),
+            pltpu.VMEM((n_chunks, 2, most, total), F32),
+            pltpu.VMEM((n_chunks, n_stored, 2, most, total), BF16),
+            pltpu.VMEM((n_chunks, n_stored, 2, most, total), BF16),
+            pltpu.VMEM((n_chunks, n_stored, most, total), BF16),
             pltpu.VMEM((total, down_weight.shape[1]), F32),
             pltpu.VMEM((n_chips, total, lane_w), F32),
             pltpu.VMEM((n_chips, total, lane_w), F32),
             pltpu.VMEM((n_chips, total, lane_w), F32),
             pltpu.VMEM((n_chips, total, lane_w), BF16),
             pltpu.VMEM((n_chips, total, lane_w), BF16),
-            dma((3, LOADS)),
+            dma((3, n_chunks)),
             dma((n_stored,)), dma((n_stored,)),
             dma((n_chips,)), dma((n_chips,)),
             dma((n_chips,)), dma((n_chips,)),
@@ -250,7 +254,7 @@
         ],
         compiler_params=pltpu.CompilerParams(
             collective_id=0, has_side_effects=True, vmem_limit_bytes=62 * 2**20),
-    )(tok, gate_weight, up_weight, down_weight)
+    )(tok, gate_weight.T, up_weight.T, down_weight)
 
 
 def solution(mesh):

time: 103 us -> 65.8 us (0.64)
  local copies, waits for them, and re-layouts: 41.2 us -> 3.04 us
  Pallas kernels: 60.6 us -> 62.5 us
    unnamed x3 -> x1, local copies, waits for them, and re-layouts: 39.7 us -> 1.47 us
    pallas_call x1, Pallas kernels: 60.6 us -> 62.5 us  [body(): pl.pallas_call(functools.partial(kernel, n_tensor, n_stored, pieces), out...]
where the time goes in v2:
time: 65.8 us; the launch traced here: 65.6 us
  Pallas kernels  62.5 us (95%)
  local copies, waits for them, and re-layouts  3.04 us (5%)
    pallas_call x1, Pallas kernels, body(): pl.pallas_call(functools.partial(kernel, n_tensor, n_stored, pieces), out...  62.5 us
    unnamed x1, local copies, waits for them, and re-layouts  1.47 us

profile of v2, /device:TPU:0, one launch (start us, length us, event | category | flops | bytes accessed | tf_op | source)
XLA Modules:
  0.0 65.6 jit_solution(11291548929111576903)
XLA Ops:
  0.0 0.9 %reshape.6 = bf16[4,4,4,512]{3,2,1,0:T(4,128)(2,1)S(1)} reshape(bf16[4,8192]{1,0:T(4,128)(2,1)} %param.4) | data formatting | bytes 131072 | tf_op jit(solution)/shard_map/reshape | solution.py:217
  0.9 0.6 reshape.7.tok_ref
  1.6 62.5 %shard_map.46 = bf16[128,256]{1,0:T(8,128)(2,1)} custom-call(bf16[4,16,512]{2,1,0:T(8,128)(2,1)} %reshape.7.tok_ref, bf16[3696,2048]{1,0:T(8,128)(2,1)} %bitcast.5, bf16[3696,2048]{1,0:T(8,128)(2,1)} %bitcast.6, bf16[3696,2048]{1,0:T(8,128)(2,1)} %down_hbm.1), custom_call_target="tpu_custom_call" | custom-call | tf_op jit(solution)/shard_map/pallas_call | solution.py:224
  64.1 1.5 %copy.9 = bf16[128,256]{1,0:T(8,128)(2,1)} copy(bf16[128,256]{1,0:T(8,128)(2,1)} %shard_map.46) | data formatting | bytes 131072
  (1 shorter events, 0.0 us)
